TPU v7x, 256 devices: a whole 4x4x8 slice. The times are simulated.
256 devices in a mesh: heads: 4 (over x_hi, core), ctx: 64 (over x_lo, z, y).
Axes of the slice: x: 4 (x_hi: 2, x_lo: 2; x = x_hi * 2 + x_lo), y: 4, z: 8, core: 2. Of those that a mesh axis runs over, the one named last changes fastest.
Arguments:
- queries: bfloat16 [12288, 2048], P('ctx', 'heads'), may hold values from -6 to 6
- key_states: bfloat16 [12288, 512], P('ctx', 'heads'), may hold values from -6 to 6
- value_states: bfloat16 [12288, 512], P('ctx', 'heads'), may hold values from -6 to 6
- attention_out: bfloat16 [12288, 2048], P('ctx', 'heads'), may hold values from -2 to 2
- out_grad: bfloat16 [12288, 2048], P('ctx', 'heads'), may hold values from -6 to 6
- log_sum_exp: float32 [16, 12288], P('heads', 'ctx'), may hold values from 0 to 16, as said below
- block_counts: int32 [64], replicated, may hold values from 1 to 3, as said below
- w_query: bfloat16 [4096, 2048], P(None, 'heads'), may hold values from -0.09375 to 0.09375
- w_key: bfloat16 [4096, 512], P(None, 'heads'), may hold values from -0.09375 to 0.09375
- w_value: bfloat16 [4096, 512], P(None, 'heads'), may hold values from -0.09375 to 0.09375
Outputs:
- input_grad: bfloat16 [12288, 4096], P('ctx', 'heads')
- key_grad: float32 [12288, 512], P('ctx', 'heads')
- value_grad: float32 [12288, 512], P('ctx', 'heads')
Inputs may be any that keep to these rules, and one draw needn't show every extreme that they name: `block_counts`: one entry equals 3. `log_sum_exp`: finite offsets of each row's scores.
All inputs are finite; a program needn't handle non-finite values.
Results may differ from a plain program's by a relative error of at most 0.0063.
Values may be sent and summed in bfloat16 or wider, within the bound.
A program may use at most 128 MiB of HBM per device.

v0:
```python
import math

import jax
import jax.numpy as jnp
from jax import lax
from jax.sharding import PartitionSpec as P

BLOCK = 64


def in_one_piece(arrays, axis, dim, along):
    widths = [a.shape[along] for a in arrays]
    both = jnp.concatenate(arrays, axis=along)
    result = lax.all_gather(both, axis, axis=dim, tiled=True)
    return tuple(jnp.split(result, [sum(widths[:k]) for k in range(1, len(widths))], axis=along))


def in_one_piece_2(arrays, axis, dim, along):
    both = jnp.concatenate(arrays, axis=along)
    result, at, done = (lax.psum_scatter(both, axis, scatter_dimension=dim, tiled=True), 0, [])
    for a in arrays:
        done.append(lax.slice_in_dim(result, at, at + a.shape[along], axis=along))
        at += a.shape[along]
    return tuple(done)


def key_span(row_count, capacity):
    shards = row_count // capacity
    per_step = max(1, min(shards, 512 // capacity))
    while shards % per_step:
        per_step = per_step - 1
    return per_step * capacity


def row_info(row_index, lengths, offsets, capacity):
    device = row_index // capacity
    onehot = device[:, None] == jnp.arange(lengths.shape[0], dtype=jnp.int32)[None, :]
    length = jnp.sum(jnp.where(onehot, lengths[None, :], 0), axis=1)
    offset = jnp.sum(jnp.where(onehot, offsets[None, :], 0), axis=1)
    within = row_index - device * capacity
    return (offset + within, within < length)


def tile_grads(
    query_blk,
    grad_blk,
    norm_blk,
    delta_blk,
    query_pos,
    query_live,
    key_blk,
    value_blk,
    key_pos,
    key_live,
    score_scale,
):
    scores = (
        jnp.einsum("qgd,kd->gqk", query_blk, key_blk, preferred_element_type=jnp.float32)
        * score_scale
    )
    visible = query_live[:, None] & key_live[None, :] & (key_pos[None, :] <= query_pos[:, None])
    probability = jnp.where(visible[None], jnp.exp(scores - norm_blk.T[:, :, None]), 0.0)
    prob_grad = jnp.einsum("qgd,kd->gqk", grad_blk, value_blk, preferred_element_type=jnp.float32)
    score_grad = probability * (prob_grad - delta_blk.T[:, :, None])
    return (probability.astype(jnp.bfloat16), score_grad.astype(jnp.bfloat16))


def on_device(
    queries,
    key_states,
    value_states,
    attention_out,
    out_grad,
    log_sum_exp,
    block_counts,
    w_query,
    w_key,
    w_value,
):
    capacity = key_states.shape[0]
    head_dim = key_states.shape[1]
    group = queries.shape[1] // head_dim
    score_scale = 1.0 / math.sqrt(head_dim)
    own_index = lax.axis_index("ctx")
    lengths = block_counts * BLOCK
    offsets = jnp.cumsum(lengths) - lengths
    own_rows = own_index * capacity + jnp.arange(capacity, dtype=jnp.int32)
    own_pos, own_live = row_info(own_rows, lengths, offsets, capacity)
    query_heads = queries.reshape(capacity, group, head_dim)
    grad_heads = out_grad.reshape(capacity, group, head_dim)
    output_heads = attention_out.reshape(capacity, group, head_dim)
    delta_rows = jnp.sum(grad_heads.astype(jnp.float32) * output_heads.astype(jnp.float32), axis=2)
    norm_rows = log_sum_exp.T
    zero_rows = jnp.zeros((capacity, group, head_dim), jnp.float32)
    rows_all = capacity * lax.axis_size("ctx")
    zero_keys = jnp.zeros((rows_all, head_dim), jnp.float32)
    key_piece, value_piece = in_one_piece((key_states, value_states), "ctx", 0, 1)
    span = key_span(key_piece.shape[0], capacity)

    def step(block_num, state):
        query_grad, key_acc, value_acc = state
        begin_row = block_num * span
        key_blk = lax.dynamic_slice_in_dim(key_piece, begin_row, span, 0)
        value_blk = lax.dynamic_slice_in_dim(value_piece, begin_row, span, 0)
        key_pos, key_live = row_info(
            begin_row + jnp.arange(span, dtype=jnp.int32), lengths, offsets, capacity
        )
        prob_b, grad_b = tile_grads(
            query_heads,
            grad_heads,
            norm_rows,
            delta_rows,
            own_pos,
            own_live,
            key_blk,
            value_blk,
            key_pos,
            key_live,
            score_scale,
        )
        key_acc = lax.dynamic_update_slice_in_dim(
            key_acc,
            score_scale
            * jnp.einsum("gqk,qgd->kd", grad_b, query_heads, preferred_element_type=jnp.float32),
            begin_row,
            0,
        )
        value_acc = lax.dynamic_update_slice_in_dim(
            value_acc,
            jnp.einsum("gqk,qgd->kd", prob_b, grad_heads, preferred_element_type=jnp.float32),
            begin_row,
            0,
        )
        return (
            query_grad
            + score_scale
            * jnp.einsum("gqk,kd->qgd", grad_b, key_blk, preferred_element_type=jnp.float32),
            key_acc,
            value_acc,
        )

    query_grad, key_terms, value_terms = lax.fori_loop(
        0, key_piece.shape[0] // span, step, (zero_rows, zero_keys, zero_keys)
    )
    key_grad, value_grad = in_one_piece_2((key_terms, value_terms), "ctx", 0, 1)
    query_flat = query_grad.reshape(capacity, group * head_dim).astype(jnp.bfloat16)
    partial_input = jnp.einsum("rc,mc->rm", query_flat, w_query, preferred_element_type=jnp.float32)
    partial_input = partial_input + jnp.einsum(
        "rc,mc->rm", key_grad.astype(jnp.bfloat16), w_key, preferred_element_type=jnp.float32
    )
    partial_input = partial_input + jnp.einsum(
        "rc,mc->rm", value_grad.astype(jnp.bfloat16), w_value, preferred_element_type=jnp.float32
    )
    input_part = lax.psum_scatter(partial_input, "heads", scatter_dimension=1, tiled=True)
    return (input_part.astype(jnp.bfloat16), key_grad, value_grad)


def solution(mesh):
    return jax.shard_map(
        on_device,
        mesh=mesh,
        in_specs=(
            P("ctx", "heads"),
            P("ctx", "heads"),
            P("ctx", "heads"),
            P("ctx", "heads"),
            P("ctx", "heads"),
            P("heads", "ctx"),
            P(),
            P(None, "heads"),
            P(None, "heads"),
            P(None, "heads"),
        ),
        out_specs=(P("ctx", "heads"), P("ctx", "heads"), P("ctx", "heads")),
        check_vma=False,
    )
```

profile of v0, /device:TPU:1, one launch (start us, length us, event | category | flops | bytes accessed | tf_op | source)
XLA Modules:
  0.0 944.5 jit_solution(15723072965911852416)
XLA Ops:
  7.2 1.6 pad_maximum_fusion.1
  14.2 262.1 %all-gather.2.cloned.1.call-done = bf16[12288,256]{1,0:T(8,128)(2,1)} async-done(((bf16[192,256]{1,0:T(8,128)(2,1)}), bf16[12288,256]{1,0:T(8,128)(2,1)}) %all-gather.2.cloned.1.call-update) | async-done | bytes 6291472 | tf_op jit(solution)/shard_map/all_gather | solution.py:14
  276.3 4.7 fusion.34
  281.0 2.8 broadcast_in_dim.142.clone
  283.8 2.8 broadcast_in_dim.142
  286.7 200.6 %while.20 = (s32[]{:T(128)}, f32[192,4,128]{2,0,1:T(8,128)S(1)}, f32[12288,128]{1,0:T(8,128)}, f32[12288,128]{1,0:T(8,128)}, bf16[12288,128]{1,0:T(8,128)(2,1)},...) while((s32[]{:T(128)}, f32[192,4,128]{2,0,1:T(8,128)S(1)}, ...), condition=%wide.region_7.8_spmd.clone, body=%wide.region_4.7_spmd.clone.sunk | while | flops 380251776 | bytes 7737797 | solution.py:142
  299.5 1.3 fusion.76
  305.7 1.3 fusion.76
  312.0 1.3 fusion.76
  324.6 1.3 fusion.76
  330.9 1.3 fusion.76
  349.7 1.3 fusion.76
  362.2 1.3 fusion.76
  424.9 1.3 fusion.76
  431.1 1.3 fusion.76
  443.6 1.3 fusion.76
  475.0 1.3 fusion.76
  487.2 10.1 %pad_maximum_fusion = f32[12288,256]{1,0:T(8,128)} fusion(f32[12288,128]{1,0:T(8,128)} %get-tuple-element.338, f32[12288,128]{1,0:T(8,128)} %get-tuple-element.337), kind=kLoop, calls=%fused_computation.39 | loop fusion | flops 3145728 | bytes 25165824 | tf_op jit(solution)/shard_map/concatenate | solution.py:19
  497.4 5.4 fusion.25
  502.8 336.0 %reduce-scatter.3.cloned.1.call-done = f32[192,256]{1,0:T(8,128)} async-done(((f32[12288,256]{1,0:T(8,128)}), f32[192,256]{1,0:T(8,128)}) %reduce-scatter.3.cloned.1.call-update) | async-done | bytes 196624 | tf_op jit(solution)/shard_map/reduce_scatter | solution.py:20
  839.8 2.5 convolution_add_fusion.1
  842.4 2.2 convolution_add_fusion
  844.7 91.4 %reduce-scatter.5.cloned.1.call-done = f32[192,1024]{1,0:T(8,128)} async-done(((f32[192,4096]{1,0:T(8,128)}), f32[192,1024]{1,0:T(8,128)}) %reduce-scatter.5.cloned.1.call-update) | async-done | bytes 786448 | tf_op jit(solution)/shard_map/reduce_scatter | solution.py:154
  936.0 1.9 convert_element_type.51
  (341 shorter events, 190.9 us)
Async XLA Ops:
  7.2 832.6 %copy-start = (bf16[4096,128]{1,0:T(8,128)(2,1)S(1)}, bf16[4096,128]{1,0:T(8,128)(2,1)}, u32[]{:S(2)}) copy-start(bf16[4096,128]{1,0:T(8,128)(2,1)} %param.20) | copy-start | bytes 3145732
  7.2 269.1 %all-gather.2.cloned.1.call-start = ((), (), s32[]{:S(2)}) async-start(), calls=%async_computation.2 | async-start | bytes 6389760 | tf_op jit(solution)/shard_map/all_gather | solution.py:14
  8.8 830.0 %reduce-scatter.3.cloned.1.call-start = ((), (), s32[]{:S(2)}) async-start(), calls=%async_computation.3 | async-start | bytes 12779520 | tf_op jit(solution)/shard_map/reduce_scatter | solution.py:20
  283.8 2.8 copy-start.4
  497.3 438.7 %reduce-scatter.5.cloned.1.call-start = ((), (), s32[]{:S(2)}) async-start(), calls=%async_computation.4 | async-start | bytes 3932160 | tf_op jit(solution)/shard_map/reduce_scatter | solution.py:154
  839.8 2.6 copy-start.3
  839.8 2.6 copy-start.2
  839.8 2.6 copy-start.1
Sparse Core Ops, SparseCore 0:
  10.3 265.8 all-gather.1
  497.5 341.2 reduce-scatter.2
  844.8 91.1 reduce-scatter.4
where the time goes:
time: 948 us; the launch traced here: 944 us
  waiting for transfers between devices  690 us (73%)
  matrix products  201 us (21%)
  other arithmetic  24.3 us (3%)
  local copies, waits for them, and re-layouts  14.7 us (2%)
  between operations  13.9 us (1%)
    reduce_scatter x1, waiting for transfers between devices, in_one_piece_2(): lax.psum_scatter(both, axis, scatter_dimension=dim, tiled=True)  336 us
    all_gather x1, waiting for transfers between devices, in_one_piece(): result = lax.all_gather(both, axis, axis=dim, tiled=True)  262 us
    reduce_scatter x1, waiting for transfers between devices, on_device(): lax.psum_scatter(partial_input, 'heads', scatter_dimension=1, tiled=True)  91.4 us
    dot_general x32, matrix products, tile_grads(): jnp.einsum('qgd,kd->gqk', query_blk, key_blk, preferred_element_type=jnp....  42.7 us
    dot_general x32, matrix products, step(): jnp.einsum('gqk,kd->qgd', grad_b, key_blk, preferred_element_type=jnp.flo...  41.6 us
    dot_general x32, matrix products, tile_grads(): jnp.einsum('qgd,kd->gqk', grad_blk, value_blk, preferred_element_type=jnp...  39 us
    dot_general x32, matrix products, step(): jnp.einsum('gqk,qgd->kd', prob_b, grad_heads, preferred_element_type=jnp....  33.7 us
    dot_general x32, matrix products, step(): jnp.einsum('gqk,qgd->kd', grad_b, query_heads, preferred_element_type=jnp...  33.4 us
  transfers between devices with their start and end apart: 3, of which 3 were waited for; matrix products, arithmetic and copies ran while one was open for 1% of the time, Pallas kernels for 0%

commit v1 on v0

v1 whole, which is shorter than its diff:
```python
import functools
import math

import jax
import jax.numpy as jnp
from jax import lax
from jax.experimental import pallas as pl
from jax.experimental.pallas import tpu as pltpu
from jax.sharding import PartitionSpec as P

UNIT = 64
CAP = 192
HD = 128
GROUP = 4
NX, NZ, NY = 2, 8, 4
CHUNK = 512
KMAX = NX * NZ * CAP + CHUNK
LOG2E = math.log2(math.e)
SCALE = 1.0 / math.sqrt(HD)
MESH = pl.DeviceIdType.MESH
VMEM = pl.BlockSpec(memory_space=pltpu.VMEM)
SMEM = pl.BlockSpec(memory_space=pltpu.SMEM)
F32 = jnp.float32
BF16 = jnp.bfloat16


def place():
    c = lax.axis_index("ctx")
    return c // (NZ * NY), lax.rem(c // NY, NZ), lax.rem(c, NY)


def ctx_id(x, z, y):
    return {"ctx": (x * NZ + z) * NY + y}


def move(src, dst, send, recv, to):
    return pltpu.make_async_remote_copy(
        src_ref=src, dst_ref=dst, send_sem=send, recv_sem=recv, device_id=to, device_id_type=MESH
    )


def greet(peers):
    barrier = pltpu.get_barrier_semaphore()
    for peer in peers:
        pl.semaphore_signal(barrier, inc=1, device_id=peer, device_id_type=MESH)
    pl.semaphore_wait(barrier, len(peers))


def neighbours(x, z, y):
    return [
        ctx_id(x, lax.rem(z + 1, NZ), y),
        ctx_id(x, lax.rem(z + NZ - 1, NZ), y),
        ctx_id(x, z, lax.rem(y + 1, NY)),
        ctx_id(x, z, lax.rem(y + NY - 1, NY)),
        ctx_id(1 - x, z, y),
    ]


DIRS = (1, -1)
CROSS = (0, 1, -1, 2, -2)


def gather_kernel(
    k_ref, v_ref, q_ref, g_ref, st_ref, kv_out, q_out, g_out, st_out,
    zs, zr, es, er, xs, xr, ys, yr,
):
    x, z, y = place()
    greet(neighbours(x, z, y))
    own = (k_ref, v_ref)

    def zz(k):
        return lax.rem(z + k + NZ, NZ)

    def ring(d, p, s):
        slot = x * NZ + zz(-DIRS[d] * s)
        src = own[p] if s == 0 else kv_out.at[slot, p]
        return move(src, kv_out.at[slot, p], zs.at[d, p, s], zr.at[d, p, s], ctx_id(x, zz(DIRS[d]), y))

    def extra(d, p, s):
        slot = zz(-DIRS[d] * s)
        return move(
            kv_out.at[slot, p], kv_out.at[slot, p], es.at[d, p, s - 2], er.at[d, p, s - 2],
            ctx_id(1, zz(DIRS[d]), y),
        )

    def cross(i, p):
        slot = zz(CROSS[i])
        src = own[p] if i == 0 else kv_out.at[slot, p]
        return move(src, kv_out.at[slot, p], xs.at[i, p], xr.at[i, p], ctx_id(1, z, y))

    def received(i, p):
        slot = zz(CROSS[i])
        return move(kv_out.at[slot, p], kv_out.at[slot, p], xs.at[i, p], xr.at[i, p], ctx_id(0, z, y))

    sources = (q_ref, g_ref, st_ref)
    targets = (q_out, g_out, st_out)

    def yy(k):
        return lax.rem(y + k + NY, NY)

    def side(d, a):
        return move(
            sources[a], targets[a].at[y], ys.at[d, a, 0], yr.at[d, a, 0], ctx_id(x, z, yy(DIRS[d]))
        )

    def far(d, a):
        slot = yy(-DIRS[d])
        return move(
            targets[a].at[slot], targets[a].at[slot], ys.at[d, a, 1], yr.at[d, a, 1],
            ctx_id(x, z, yy(DIRS[d])),
        )

    def valid(d, p, s):
        return s < 3 or d == p

    for p in range(2):
        for d in range(2):
            ring(d, p, 0).start()

    @pl.when(x == 0)
    def _():
        for p in range(2):
            cross(0, p).start()

    side(0, 0).start()
    side(1, 1).start()
    side(0, 2).start()
    side(1, 0).start()
    side(0, 1).start()
    side(1, 2).start()
    kv_out[x * NZ + z, 0] = k_ref[...]
    kv_out[x * NZ + z, 1] = v_ref[...]
    q_out[y] = q_ref[...]
    g_out[y] = g_ref[...]
    st_out[y] = st_ref[...]

    for s in range(1, 3):
        for p in range(2):
            for d in range(2):
                ring(d, p, s - 1).wait_recv()
                ring(d, p, s).start() if valid(d, p, s) else None

                @pl.when(x == 0)
                def _():
                    cross(CROSS.index(-DIRS[d] * s), p).start()

    side(0, 0).wait_recv()
    far(0, 0).start()
    side(1, 1).wait_recv()
    far(1, 1).start()
    side(0, 2).wait_recv()
    far(0, 2).start()
    for p in range(2):
        for d in range(2):
            ring(d, p, 2).wait_recv()
            if valid(d, p, 3):
                ring(d, p, 3).start()

    @pl.when(x == 1)
    def _():
        for p in range(2):
            for d in range(2):
                received(CROSS.index(-DIRS[d] * 2), p).wait_recv()
                extra(d, p, 2).start()
        for p in range(2):
            for d in range(2):
                extra(d, p, 2).wait_recv()
                if valid(d, p, 3):
                    extra(d, p, 3).start()
        for p in range(2):
            for i in range(3):
                received(i, p).wait_recv()
        for p in range(2):
            extra(p, p, 3).wait_recv()

    for p in range(2):
        ring(p, p, 3).wait_recv()
    side(1, 0).wait_recv()
    side(0, 1).wait_recv()
    side(1, 2).wait_recv()
    far(0, 0).wait_recv()
    far(1, 1).wait_recv()
    far(0, 2).wait_recv()

    for s in range(4):
        for p in range(2):
            for d in range(2):
                if valid(d, p, s):
                    ring(d, p, s).wait_send()
    for d in range(2):
        for a in range(3):
            side(d, a).wait_send()
    far(0, 0).wait_send()
    far(1, 1).wait_send()
    far(0, 2).wait_send()

    @pl.when(x == 0)
    def _():
        for p in range(2):
            for i in range(5):
                cross(i, p).wait_send()

    @pl.when(x == 1)
    def _():
        for p in range(2):
            for d in range(2):
                extra(d, p, 2).wait_send()
            extra(p, p, 3).wait_send()


def gather(k, v, q, g, st):
    dma = pltpu.SemaphoreType.DMA
    return pl.pallas_call(
        gather_kernel,
        name="gather_blocks",
        out_shape=(
            jax.ShapeDtypeStruct((NX * NZ, 2, CAP, HD), BF16),
            jax.ShapeDtypeStruct((NY, CAP, GROUP * HD), BF16),
            jax.ShapeDtypeStruct((NY, CAP, GROUP * HD), BF16),
            jax.ShapeDtypeStruct((NY, 8, GROUP * UNIT), F32),
        ),
        in_specs=[VMEM] * 5,
        out_specs=(VMEM,) * 4,
        scratch_shapes=[
            dma((2, 2, 4)), dma((2, 2, 4)), dma((2, 2, 2)), dma((2, 2, 2)),
            dma((5, 2)), dma((5, 2)), dma((2, 3, 2)), dma((2, 3, 2)),
        ],
        compiler_params=pltpu.CompilerParams(collective_id=0, has_side_effects=True),
    )(k, v, q, g, st)


def dot(a, b, dims):
    return lax.dot_general(a, b, (dims, ((), ())), preferred_element_type=F32)


def attention_kernel(
    count_ref, kv_ref, q_ref, g_ref, st_ref, dkv_out, dq_out, kc, vc, kt, dk, dv, dqt, starts
):
    x, z, y = place()
    mine = x * NZ + z

    def block_of(j):
        return j * NY + y

    def pack(j, n):
        starts[j] = n
        at = pl.ds(pl.multiple_of(n * UNIT, UNIT), CAP)
        kc[at, :] = kv_ref[j, 0]
        vc[at, :] = kv_ref[j, 1]
        return n + count_ref[block_of(j)]

    total = lax.fori_loop(0, mine + 1, pack, 0)
    tail = pl.ds(pl.multiple_of(total * UNIT, UNIT), CHUNK)
    kc[tail, :] = jnp.zeros((CHUNK, HD), BF16)
    vc[tail, :] = jnp.zeros((CHUNK, HD), BF16)
    chunks = (total * UNIT + CHUNK - 1) // CHUNK

    @pl.loop(0, chunks)
    def _(ci):
        rows = pl.ds(pl.multiple_of(ci * CHUNK, CHUNK), CHUNK)
        kt[ci] = kc[rows, :].T
        dk[rows, :] = jnp.zeros((CHUNK, HD), F32)
        dv[rows, :] = jnp.zeros((CHUNK, HD), F32)

    before = starts[mine]
    lane = lax.rem(lax.broadcasted_iota(jnp.int32, (1, GROUP * UNIT), 1), UNIT)
    heads = [slice(h * HD, (h + 1) * HD) for h in range(GROUP)]

    @pl.loop(0, NY)
    def _(b):
        live = count_ref[mine * NY + b]
        dq_out[b] = jnp.zeros((CAP, GROUP * HD), BF16)

        @pl.loop(0, live)
        def _(u):
            at = pl.ds(pl.multiple_of(u * UNIT, UNIT), UNIT)
            qn = jnp.concatenate([q_ref[b, at, h] for h in heads], axis=0)
            gn = jnp.concatenate([g_ref[b, at, h] for h in heads], axis=0)
            norm = st_ref[b, pl.ds(u, 1), :]
            delta = st_ref[b, pl.ds(u + 4, 1), :]
            here = jnp.where(b > y, count_ref[block_of(mine)], jnp.where(b == y, u + 1, 0))
            seen = before + here
            limit = (seen - 1) * UNIT + jnp.where(b == y, lane, UNIT - 1)
            dqt[...] = jnp.zeros_like(dqt)

            def step(ci, masked):
                for half in range(CHUNK // 256):
                    first = ci * CHUNK + half * 256
                    rows = pl.ds(pl.multiple_of(first, 256), 256)
                    s = dot(kc[rows, :], qn, ((1,), (1,)))
                    prob = jnp.exp2(s * (SCALE * LOG2E) - norm)
                    if masked:
                        key = first + lax.broadcasted_iota(jnp.int32, prob.shape, 0)
                        prob = jnp.where(key <= limit, prob, 0.0)
                    dp = dot(vc[rows, :], gn, ((1,), (1,)))
                    ds = (prob * (dp - delta)).astype(BF16)
                    dv[rows, :] += dot(prob.astype(BF16), gn, ((1,), (0,)))
                    dk[rows, :] += dot(ds, qn, ((1,), (0,)))
                    dqt[...] += dot(kt[ci, :, half * 256:(half + 1) * 256], ds, ((1,), (0,)))

            full = jnp.maximum(seen - 1, 0) * UNIT // CHUNK
            whole = (seen * UNIT + CHUNK - 1) // CHUNK

            @pl.loop(0, full)
            def _(ci):
                step(ci, False)

            @pl.loop(full, whole)
            def _(ci):
                step(ci, True)

            dq = (dqt[...].T * SCALE).astype(BF16)
            for i, h in enumerate(heads):
                dq_out[b, at, h] = dq[i * UNIT:(i + 1) * UNIT]

    @pl.loop(0, NX * NZ)
    def _(j):
        @pl.when(j <= mine)
        def _():
            at = pl.ds(pl.multiple_of(starts[j] * UNIT, UNIT), CAP)
            row = lax.broadcasted_iota(jnp.int32, (CAP, HD), 0)
            keep = row < count_ref[block_of(j)] * UNIT
            dkv_out[j, 0] = jnp.where(keep, dk[at, :] * SCALE, 0.0).astype(BF16)
            dkv_out[j, 1] = jnp.where(keep, dv[at, :], 0.0).astype(BF16)

        @pl.when(j > mine)
        def _():
            dkv_out[j] = jnp.zeros((2, CAP, HD), BF16)


def attention(counts, kv, q, g, st):
    return pl.pallas_call(
        attention_kernel,
        name="attention_grads",
        out_shape=(
            jax.ShapeDtypeStruct((NX * NZ, 2, CAP, HD), BF16),
            jax.ShapeDtypeStruct((NY, CAP, GROUP * HD), BF16),
        ),
        in_specs=[SMEM] + [VMEM] * 4,
        out_specs=(VMEM,) * 2,
        scratch_shapes=[
            pltpu.VMEM((KMAX, HD), BF16),
            pltpu.VMEM((KMAX, HD), BF16),
            pltpu.VMEM((KMAX // CHUNK, HD, CHUNK), BF16),
            pltpu.VMEM((KMAX, HD), F32),
            pltpu.VMEM((KMAX, HD), F32),
            pltpu.VMEM((HD, GROUP * UNIT), F32),
            pltpu.SMEM((NX * NZ,), jnp.int32),
        ],
    )(counts, kv, q, g, st)


def reduce_kernel(
    p_ref, q_ref, dk_out, dv_out, dq_out,
    zst, zrb, est, erb, xst, xrb, yst, yrb, fst,
    zs, zr, es, er, xs, xr, ys, yr, fs, fr,
):
    x, z, y = place()
    greet(neighbours(x, z, y))

    def zz(k):
        return lax.rem(z + k + NZ, NZ)

    def yy(k):
        return lax.rem(y + k + NY, NY)

    def valid(d, p, s):
        return s > 0 or d == p

    def part(row, d, s, p):
        return p_ref.at[row * NZ + zz(DIRS[d] * (4 - s)), p]

    def joins(d, p, s):
        return s > 0 and valid(d, p, s - 1)

    def ring(d, p, s, src=None):
        src = zst.at[d, p, s] if src is None else src
        return move(src, zrb.at[d, p, s], zs.at[d, p, s], zr.at[d, p, s], ctx_id(x, zz(DIRS[d]), y))

    def extra(d, p, s, src=None):
        src = est.at[d, p, s] if src is None else src
        return move(src, erb.at[d, p, s], es.at[d, p, s], er.at[d, p, s], ctx_id(1, zz(DIRS[d]), y))

    def cross(i, p, src=None):
        src = xst.at[i - 3, p] if src is None else src
        return move(src, xrb.at[i, p], xs.at[i, p], xr.at[i, p], ctx_id(0, z, y))

    def crossed(i, p):
        return move(xrb.at[i, p], xrb.at[i, p], xs.at[i, p], xr.at[i, p], ctx_id(1, z, y))

    half = CAP // 2
    rows = (slice(0, half), slice(half, CAP))

    def far(d):
        return move(
            q_ref.at[yy(2), rows[d]], fst.at[d], fs.at[d], fr.at[d], ctx_id(x, z, yy(DIRS[d]))
        )

    def side(d, joined):
        r = d if joined else 1 - d
        src = yst.at[d] if joined else q_ref.at[yy(DIRS[d]), rows[r]]
        return move(
            src, yrb.at[d, rows[r]], ys.at[d, r], yr.at[d, r], ctx_id(x, z, yy(DIRS[d]))
        )

    for d in range(2):
        ring(d, d, 0, part(x, d, 0, d)).start()

        @pl.when(x == 1)
        def _():
            extra(d, d, 0, part(0, d, 0, d)).start()

        ring(d, 1 - d, 1, part(x, d, 1, 1 - d)).start()

        @pl.when(x == 1)
        def _():
            extra(d, 1 - d, 1, part(0, d, 1, 1 - d)).start()

        far(d).start()

    @pl.when(x == 1)
    def _():
        for p in range(2):
            for i in range(3):
                cross(i, p, p_ref.at[zz(CROSS[i]), p]).start()

    for d in range(2):
        side(d, False).start()

    def add(*refs):
        total = refs[0][...].astype(F32)
        for r in refs[1:]:
            total = total + r[...].astype(F32)
        return total

    for d in range(2):
        @pl.when(x == 1)
        def _():
            extra(d, d, 0, part(0, d, 0, d)).wait_recv()
            est[d, d, 1] = add(part(0, d, 1, d), erb.at[d, d, 0]).astype(BF16)
            extra(d, d, 1).start()

        ring(d, d, 0, part(x, d, 0, d)).wait_recv()
        zst[d, d, 1] = add(part(x, d, 1, d), zrb.at[d, d, 0]).astype(BF16)
        ring(d, d, 1).start()

    @pl.when(x == 1)
    def _():
        for p in range(2):
            for d in range(2):
                i = CROSS.index(2 * DIRS[d])
                extra(d, p, 1).wait_recv()
                xst[i - 3, p] = add(part(0, d, 2, p), erb.at[d, p, 1]).astype(BF16)
                cross(i, p).start()

    for d in range(2):
        far(d).wait_recv()
        yst[d] = add(q_ref.at[yy(DIRS[d]), rows[d]], fst.at[d]).astype(BF16)
        side(d, True).start()

    for s in range(2, 4):
        for p in range(2):
            for d in range(2):
                ring(d, p, s - 1).wait_recv()

                @pl.when(x == 0)
                def _():
                    i = CROSS.index((4 - s) * DIRS[d])
                    crossed(i, p).wait_recv()
                    zst[d, p, s] = add(part(x, d, s, p), zrb.at[d, p, s - 1], xrb.at[i, p]).astype(BF16)

                @pl.when(x == 1)
                def _():
                    zst[d, p, s] = add(part(x, d, s, p), zrb.at[d, p, s - 1]).astype(BF16)

                ring(d, p, s).start()

    for d in range(2):
        side(d, False).wait_recv()
        side(d, True).wait_recv()
    dq_out[...] = add(q_ref.at[y], yrb.at[0], yrb.at[1]).astype(BF16)

    outs = (dk_out, dv_out)
    for p in range(2):
        for d in range(2):
            ring(d, p, 3).wait_recv()

        @pl.when(x == 0)
        def _():
            crossed(0, p).wait_recv()
            outs[p][...] = add(p_ref.at[z, p], zrb.at[0, p, 3], zrb.at[1, p, 3], xrb.at[0, p])

        @pl.when(x == 1)
        def _():
            outs[p][...] = add(p_ref.at[NZ + z, p], zrb.at[0, p, 3], zrb.at[1, p, 3])

    for p in range(2):
        for d in range(2):
            for s in range(4):
                if valid(d, p, s):
                    ring(d, p, s).wait_send()

        @pl.when(x == 1)
        def _():
            for d in range(2):
                for s in range(2):
                    if valid(d, p, s):
                        extra(d, p, s).wait_send()
            for i in range(5):
                cross(i, p, xrb.at[i, p]).wait_send()

    for d in range(2):
        far(d).wait_send()
        side(d, False).wait_send()
        side(d, True).wait_send()


def reduce_blocks(parts, q_parts):
    dma = pltpu.SemaphoreType.DMA
    tile = (CAP, HD)
    return pl.pallas_call(
        reduce_kernel,
        name="reduce_blocks",
        out_shape=(
            jax.ShapeDtypeStruct(tile, F32),
            jax.ShapeDtypeStruct(tile, F32),
            jax.ShapeDtypeStruct((CAP, GROUP * HD), BF16),
        ),
        in_specs=[VMEM] * 2,
        out_specs=(VMEM,) * 3,
        scratch_shapes=[
            pltpu.VMEM((2, 2, 4) + tile, BF16),
            pltpu.VMEM((2, 2, 4) + tile, BF16),
            pltpu.VMEM((2, 2, 2) + tile, BF16),
            pltpu.VMEM((2, 2, 2) + tile, BF16),
            pltpu.VMEM((2, 2) + tile, BF16),
            pltpu.VMEM((5, 2) + tile, BF16),
            pltpu.VMEM((2, CAP // 2, GROUP * HD), BF16),
            pltpu.VMEM((2, CAP, GROUP * HD), BF16),
            pltpu.VMEM((2, CAP // 2, GROUP * HD), BF16),
            dma((2, 2, 4)), dma((2, 2, 4)), dma((2, 2, 2)), dma((2, 2, 2)),
            dma((5, 2)), dma((5, 2)), dma((2, 2)), dma((2, 2)), dma((2,)), dma((2,)),
        ],
        compiler_params=pltpu.CompilerParams(collective_id=1, has_side_effects=True),
    )(parts, q_parts)


def heads_kernel(
    p_ref, out_ref, near, farb, stage, relay, last, cs, cr, rs, rr, ls, lr
):
    hd = lax.axis_index("heads")
    x_lo, z, y = place()
    x_hi, core = hd // 2, lax.rem(hd, 2)
    xx = x_hi * 2 + x_lo
    width = out_ref.shape[1]

    def device(k):
        to = lax.rem(xx + k + 4, 4)
        return {"heads": (to // 2) * 2 + core, **ctx_id(lax.rem(to, 2), z, y)}

    partner = {"heads": x_hi * 2 + 1 - core}
    greet([partner, device(1), device(-1)])

    def columns(hi, c):
        return pl.ds(pl.multiple_of((hi * 2 + c) * width, width), width)

    pieces = 4
    height = CAP // pieces
    rows = [pl.ds(i * height, height) for i in range(pieces)]

    def swap(i, which):
        hi = 1 - x_hi if which == 0 else x_hi
        dst = farb if which == 0 else near
        return move(
            p_ref.at[rows[i], columns(hi, 1 - core)], dst.at[rows[i]], cs.at[which, i], cr.at[which, i], partner
        )

    def hop(i):
        d = DIRS[i % 2]
        return move(stage.at[rows[i]], relay.at[rows[i]], rs.at[i], rr.at[i], device(d))

    def forward(i):
        d = DIRS[i % 2]
        return move(relay.at[rows[i]], last.at[rows[i]], ls.at[i], lr.at[i], device(d))

    for which in range(2):
        for i in range(pieces):
            swap(i, which).start()
    for i in range(pieces):
        swap(i, 0).wait_recv()
        own = p_ref[rows[i], columns(1 - x_hi, core)].astype(F32)
        stage[rows[i]] = (own + farb[rows[i]].astype(F32)).astype(BF16)
        hop(i).start()
    for i in range(pieces):
        hop(i).wait_recv()
        forward(i).start()
    for i in range(pieces):
        swap(i, 1).wait_recv()
    for i in range(pieces):
        forward(i).wait_recv()
        own = p_ref[rows[i], columns(x_hi, core)].astype(F32)
        out_ref[rows[i]] = (own + near[rows[i]].astype(F32) + last[rows[i]].astype(F32)).astype(BF16)
    for i in range(pieces):
        swap(i, 0).wait_send()
        swap(i, 1).wait_send()
        hop(i).wait_send()
        forward(i).wait_send()


def sum_heads(partial):
    dma = pltpu.SemaphoreType.DMA
    block = (CAP, partial.shape[1] // 4)
    return pl.pallas_call(
        heads_kernel,
        name="sum_heads",
        out_shape=jax.ShapeDtypeStruct(block, BF16),
        in_specs=[VMEM],
        out_specs=VMEM,
        scratch_shapes=[pltpu.VMEM(block, BF16)] * 5
        + [dma((2, 4)), dma((2, 4)), dma((4,)), dma((4,)), dma((4,)), dma((4,))],
        compiler_params=pltpu.CompilerParams(collective_id=2, has_side_effects=True),
    )(partial)


def on_device(q, k, v, o, g, lse, counts, wq, wk, wv):
    per_unit = CAP // UNIT
    delta = jnp.sum((g.astype(F32) * o.astype(F32)).reshape(CAP, GROUP, HD), axis=2)
    delta = delta.reshape(per_unit, UNIT, GROUP).transpose(0, 2, 1).reshape(per_unit, GROUP * UNIT)
    norm = (lse * LOG2E).reshape(GROUP, per_unit, UNIT).transpose(1, 0, 2)
    norm = norm.reshape(per_unit, GROUP * UNIT)
    gap = jnp.zeros((1, GROUP * UNIT), F32)
    st = jnp.concatenate([norm, gap, delta, gap], axis=0)
    kv_all, q_all, g_all, st_all = gather(k, v, q, g, st)
    parts, q_parts = attention(counts, kv_all, q_all, g_all, st_all)
    dk, dv, dq = reduce_blocks(parts, q_parts)
    mul = functools.partial(jnp.einsum, "rc,mc->rm", preferred_element_type=F32)
    partial = mul(dq, wq) + mul(dk.astype(BF16), wk) + mul(dv.astype(BF16), wv)
    return sum_heads(partial.astype(BF16)), dk, dv


def solution(mesh):
    return jax.shard_map(
        on_device,
        mesh=mesh,
        in_specs=(
            P("ctx", "heads"), P("ctx", "heads"), P("ctx", "heads"), P("ctx", "heads"), P("ctx", "heads"),
            P("heads", "ctx"), P(), P(None, "heads"), P(None, "heads"), P(None, "heads"),
        ),
        out_specs=(P("ctx", "heads"), P("ctx", "heads"), P("ctx", "heads")),
        check_vma=False,
    )
```

time: 948 us -> 118 us (0.12)
  waiting for transfers between devices: 690 us -> 0 us
  matrix products: 201 us -> 6.15 us
  Pallas kernels: 0 us -> 105 us
  other arithmetic: 24.3 us -> 2.75 us
  between operations: 13.9 us -> 0.75 us
  local copies, waits for them, and re-layouts: 14.7 us -> 4.18 us
    reduce_scatter x2 -> x0, waiting for transfers between devices: 427 us -> none  [the longest x1 336 us: in_one_piece_2(): lax.psum_scatter(both, axis, scatter_dimension=dim, tiled=True)]
    all_gather x1 -> x0, waiting for transfers between devices: 262 us -> none  [in_one_piece(): result = lax.all_gather(both, axis, axis=dim, tiled=True)]
    dot_general x163 -> x3, matrix products: 201 us -> 6.15 us  [on_device(): partial = mul(dq, wq) + mul(dk.astype(BF16), wk) + mul(dv.astype(BF16), wv)]
    pallas_call x0 -> x4, Pallas kernels: none -> 105 us  [the longest x1 48.3 us: reduce_blocks(): pl.pallas_call(reduce_kernel, name='reduce_blocks', out_shape=(jax.ShapeD...]
    concatenate x2 -> x1, other arithmetic: 11.6 us -> 0.63 us  [on_device(): st = jnp.concatenate([norm, gap, delta, gap], axis=0)]
  transfers between devices with their start and end apart: 3 -> 0, of which waited for: 3 -> 0; matrix products, arithmetic and copies ran while one was open for 1% -> 0% of each run, Pallas kernels for 0% -> 0%
where the time goes in v1:
time: 118 us; the launch traced here: 119 us
  Pallas kernels  105 us (89%)
  matrix products  6.15 us (5%)
  local copies, waits for them, and re-layouts  4.18 us (4%)
  other arithmetic  2.75 us (2%)
    pallas_call x1, Pallas kernels, reduce_blocks(): pl.pallas_call(reduce_kernel, name='reduce_blocks', out_shape=(jax.ShapeD...  48.3 us
    pallas_call x1, Pallas kernels, gather(): pl.pallas_call(gather_kernel, name='gather_blocks', out_shape=(jax.ShapeD...  25.9 us
    pallas_call x1, Pallas kernels, sum_heads(): pl.pallas_call(heads_kernel, name='sum_heads', out_shape=jax.ShapeDtypeSt...  21 us
    pallas_call x1, Pallas kernels, attention(): pl.pallas_call(attention_kernel, name='attention_grads', out_shape=(jax.S...  9.52 us
    dot_general x3, matrix products, on_device(): partial = mul(dq, wq) + mul(dk.astype(BF16), wk) + mul(dv.astype(BF16), wv)  6.15 us
    unnamed x11, local copies, waits for them, and re-layouts  3.7 us

profile of v1, /device:TPU:1, one launch (start us, length us, event | category | flops | bytes accessed | tf_op | source)
XLA Modules:
  0.0 118.6 jit_solution(10480889457321783865)
XLA Ops:
  0.6 0.0 copy-start
  0.6 0.8 broadcast_multiply_fusion
  1.4 0.1 reshape.21
  1.5 0.1 reshape.22
  1.6 1.1 convert_multiply_fusion
  2.7 0.1 reshape.23
  2.8 0.3 reduce_sum.9
  3.1 0.1 copy.20
  3.2 0.1 reshape.25
  3.3 0.6 pad_maximum_fusion.st_ref
  3.9 25.9 %gather_blocks.1 = (bf16[16,2,192,128]{3,2,1,0:T(8,128)(2,1)}, bf16[4,192,512]{2,1,0:T(8,128)(2,1)}, bf16[4,192,512]{2,1,0:T(8,128)(2,1)}, f32[4,8,256]{2,1,0:T(8,128)}) custom-call(bf16[192,128]{1,0:T(8,128)(2,1)} %k_ref.1, bf16[192,128]{1,0:T(8,128)(2,1)} %v_ref.1, bf16[192,512]{1,0:T(8,128)(2,1)} %q_ref.1, bf16[192,512]{1,0:T(8,128)(2,1)} %g_ref.1, ...), custom_call_target="tpu_custom_call" | custom-call | tf_op jit(solution)/shard_map/gather_blocks/pallas_call | solution.py:213
  29.8 9.5 %attention_grads.1 = (bf16[16,2,192,128]{3,2,1,0:T(8,128)(2,1)}, bf16[4,192,512]{2,1,0:T(8,128)(2,1)}) custom-call(s32[64]{0:T(128)} %count_ref.1, bf16[16,2,192,128]{3,2,1,0:T(8,128)(2,1)} %get-tuple-element.12.kv_ref, bf16[4,192,512]{2,1,0:T(8,128)(2,1)} %get-tuple-element.13.q_ref, bf16[4,192,512]{2,1,0:T(8,128)(2,1)} %get-tuple-element.14.g_ref, ...), custom_call_target="tpu_custom_call" | custom-call | tf_op jit(solution)/shard_map/attention_grads/pallas_call | solution.py:332
  39.3 48.3 %reduce_blocks.1 = (f32[192,128]{1,0:T(8,128)}, f32[192,128]{1,0:T(8,128)}, bf16[192,512]{1,0:T(8,128)(2,1)}) custom-call(bf16[16,2,192,128]{3,2,1,0:T(8,128)(2,1)} %get-tuple-element.16.p_ref, bf16[4,192,512]{2,1,0:T(8,128)(2,1)} %get-tuple-element.17.q_ref), custom_call_target="tpu_custom_call" | custom-call | tf_op jit(solution)/shard_map/reduce_blocks/pallas_call | solution.py:521
  87.6 3.8 %fusion.3 = f32[192,4096]{1,0:T(8,128)S(1)} fusion(bf16[192,512]{1,0:T(8,128)(2,1)} %get-tuple-element.18, bf16[4096,512]{1,0:T(8,128)(2,1)} %param.17), kind=kOutput, calls=%fused_computation.8 | convolution fusion | flops 805306368 | bytes 7536640 | tf_op jit(solution)/shard_map/rc,mc->rm/dot_general | solution.py:637
  91.5 0.0 copy-done
  91.5 0.0 copy-done.2
  91.5 0.0 copy-start.1
  91.5 0.6 convolution_add_fusion.1
  92.1 0.6 copy-done.1
  92.7 1.7 %fusion.p_ref = bf16[192,4096]{1,0:T(8,128)(2,1)} fusion(f32[192,4096]{1,0:T(8,128)S(1)} %convolution_add_fusion.1, bf16[4096,128]{1,0:T(8,128)(2,1)S(1)} %copy-done.1, f32[192,128]{1,0:T(8,128)S(1)} %copy-done.3), kind=kOutput, calls=%fused_computation.2 | convolution fusion | flops 202924032 | bytes 5865472 | tf_op jit(solution)/shard_map/rc,mc->rm/dot_general | solution.py:637
  94.5 21.0 %sum_heads.1 = bf16[192,1024]{1,0:T(8,128)(2,1)} custom-call(bf16[192,4096]{1,0:T(8,128)(2,1)} %fusion.p_ref), custom_call_target="tpu_custom_call" | custom-call | tf_op jit(solution)/shard_map/sum_heads/pallas_call | solution.py:613
  115.5 1.8 %copy.24 = bf16[192,1024]{1,0:T(8,128)(2,1)} copy(bf16[192,1024]{1,0:T(8,128)(2,1)} %sum_heads.1) | data formatting | bytes 786432
  117.3 0.6 copy.25
  117.9 0.6 copy.26
  (5 shorter events, 0.0 us)
Async XLA Ops:
  0.6 90.9 %copy-start = (bf16[4096,128]{1,0:T(8,128)(2,1)S(1)}, bf16[4096,128]{1,0:T(8,128)(2,1)}, u32[]{:S(2)}) copy-start(bf16[4096,128]{1,0:T(8,128)(2,1)} %param.18) | copy-start | bytes 3145732
  87.6 3.9 %copy-start.2 = (f32[192,128]{1,0:T(8,128)S(1)}, f32[192,128]{1,0:T(8,128)}, u32[]{:S(2)}) copy-start(f32[192,128]{1,0:T(8,128)} %get-tuple-element.25) | copy-start | bytes 294916
  91.5 1.2 %copy-start.1 = (bf16[4096,128]{1,0:T(8,128)(2,1)S(1)}, bf16[4096,128]{1,0:T(8,128)(2,1)}, u32[]{:S(2)}) copy-start(bf16[4096,128]{1,0:T(8,128)(2,1)} %param.19) | copy-start | bytes 3145732
  91.5 1.2 %copy-start.3 = (f32[192,128]{1,0:T(8,128)S(1)}, f32[192,128]{1,0:T(8,128)}, u32[]{:S(2)}) copy-start(f32[192,128]{1,0:T(8,128)} %get-tuple-element.26) | copy-start | bytes 294916

commit v2 on v0

v2 whole, which is shorter than its diff:
```python
import math

import jax
import jax.numpy as jnp
from jax import lax
from jax.experimental import pallas as pl
from jax.experimental.pallas import tpu as pltpu
from jax.sharding import PartitionSpec as P

UNIT = 64
CAP = 192
HD = 128
GROUP = 4
NX, NZ, NY = 2, 8, 4
TILE = 256
PIECES = 6
LOG2E = math.log2(math.e)
SCALE = 1.0 / math.sqrt(HD)
MESH = pl.DeviceIdType.MESH
VMEM = pl.BlockSpec(memory_space=pltpu.VMEM)
SMEM = pl.BlockSpec(memory_space=pltpu.SMEM)
F32 = jnp.float32
BF16 = jnp.bfloat16


def place():
    c = lax.axis_index("ctx")
    return c // (NZ * NY), lax.rem(c // NY, NZ), lax.rem(c, NY)


def ctx_id(x, z, y):
    return {"ctx": (x * NZ + z) * NY + y}


def move(src, dst, send, recv, to):
    return pltpu.make_async_remote_copy(
        src_ref=src, dst_ref=dst, send_sem=send, recv_sem=recv, device_id=to, device_id_type=MESH
    )


def greet(peers):
    barrier = pltpu.get_barrier_semaphore()
    for peer in peers:
        pl.semaphore_signal(barrier, inc=1, device_id=peer, device_id_type=MESH)
    pl.semaphore_wait(barrier, len(peers))


DIRS = (1, -1)
CROSS = (0, 1, -1, 2, -2)


def weight_copies(w_refs, buf, sems, first):
    copies = []
    for c in range(buf.shape[0]):
        rows, at, group = pl.ds(pl.multiple_of(first + c * TILE, TILE), TILE), 0, []
        for i, w in enumerate(w_refs):
            width = w.shape[1]
            group.append(pltpu.make_async_copy(w.at[rows], buf.at[c, :, at:at + width], sems.at[c, i]))
            at += width
        copies.append(group)
    for group in copies:
        for copy in group:
            copy.start()
    return copies


def dot(a, b, dims):
    return lax.dot_general(a, b, (dims, ((), ())), preferred_element_type=F32)


def fused_kernel(
    count_ref, k_ref, v_ref, q_ref, g_ref, o_ref, lse_ref, wq, wk, wv,
    out_ref, dk_out, dv_out,
    kv, qa, ga, st, kt, acc, dqt, pb, db,
    zst, zrb, est, erb, xst, xrb, fst, frb, yst, yrb,
    act, far, near, farb, nearb, stage, relay, last, wbuf,
    gz, gx, gy, sz, sx, sy, hs, wsem,
):
    hd = lax.axis_index("heads")
    x, z, y = place()
    x_hi, core = hd // 2, lax.rem(hd, 2)
    xx = x_hi * 2 + x
    width = out_ref.shape[1]
    tiles = wbuf.shape[0] // 2
    UNITS = CAP // UNIT
    own = (k_ref, v_ref)

    def zz(k):
        return lax.rem(z + k + NZ, NZ)

    def yy(k):
        return lax.rem(y + k + NY, NY)

    def device(k):
        to = lax.rem(xx + k + 4, 4)
        return {"heads": (to // 2) * 2 + core, **ctx_id(lax.rem(to, 2), z, y)}

    partner = {"heads": x_hi * 2 + 1 - core}

    def along_z(d):
        return ctx_id(x, zz(DIRS[d]), y)

    def along_y(d):
        return ctx_id(x, z, yy(DIRS[d]))

    twin = ctx_id(1 - x, z, y)
    greet([along_z(0), along_z(1), along_y(0), along_y(1), partner, device(1), device(-1)])

    def ring(d, p, s):
        slot = x * NZ + zz(-DIRS[d] * s)
        src = own[p] if s == 0 else kv.at[slot, p]
        return move(src, kv.at[slot, p], gz.at[0, 0, d, p, s], gz.at[0, 1, d, p, s], along_z(d))

    def extra(d, p, s):
        slot = zz(-DIRS[d] * s)
        return move(kv.at[slot, p], kv.at[slot, p], gz.at[1, 0, d, p, s], gz.at[1, 1, d, p, s], along_z(d))

    def cross(i, p):
        slot = zz(CROSS[i])
        src = own[p] if i == 0 else kv.at[slot, p]
        return move(src, kv.at[slot, p], gx.at[0, i, p], gx.at[1, i, p], twin)

    def crossed(i, p):
        slot = zz(CROSS[i])
        return move(kv.at[slot, p], kv.at[slot, p], gx.at[0, i, p], gx.at[1, i, p], twin)

    sources, targets = (q_ref, g_ref, st.at[y]), (qa, ga, st)

    def side(d, a):
        return move(sources[a], targets[a].at[y], gy.at[0, 0, d, a], gy.at[0, 1, d, a], along_y(d))

    def far_side(d, a):
        slot = yy(-DIRS[d])
        return move(
            targets[a].at[slot], targets[a].at[slot], gy.at[1, 0, d, a], gy.at[1, 1, d, a], along_y(d)
        )

    def valid(d, p, s):
        return s < 3 or d == p

    for p in range(2):
        for d in range(2):
            ring(d, p, 0).start()

    @pl.when(x == 0)
    def _():
        for p in range(2):
            cross(0, p).start()

    side(0, 0).start()
    side(1, 1).start()
    side(1, 0).start()
    side(0, 1).start()
    kv[x * NZ + z, 0] = k_ref[...]
    kv[x * NZ + z, 1] = v_ref[...]
    qa[y] = q_ref[...]
    ga[y] = g_ref[...]
    st[y] = jnp.zeros(st.shape[1:], F32)
    for h in range(GROUP):
        cols = slice(h * HD, (h + 1) * HD)
        both = g_ref[:, cols].astype(F32) * o_ref[:, cols].astype(F32)
        delta = jnp.sum(both.T, axis=0, keepdims=True)
        norm = lse_ref[h:h + 1, :] * LOG2E
        for u in range(UNITS):
            part = slice(u * UNIT, (u + 1) * UNIT)
            into = slice(h * UNIT, (h + 1) * UNIT)
            st[y, u:u + 1, into] = norm[:, part]
            st[y, u + 4:u + 5, into] = delta[:, part]
    side(0, 2).start()
    side(1, 2).start()
    dqt[...] = jnp.zeros_like(dqt)

    lane = lax.rem(lax.broadcasted_iota(jnp.int32, (1, GROUP * UNIT), 1), UNIT)
    key = lax.broadcasted_iota(jnp.int32, (CAP, GROUP * UNIT), 0)
    heads = [slice(h * HD, (h + 1) * HD) for h in range(GROUP)]

    def block(keys, query_blocks, fresh):
        slots = [row * NZ + zz(e) for row, e in keys]
        units = [(b, u) for b in query_blocks for u in range(UNITS)]
        if fresh:
            for slot in slots:
                kt[slot] = kv[slot, 0].T

        def operands(i):
            b, u = units[i]
            at = slice(u * UNIT, (u + 1) * UNIT)
            qn = jnp.concatenate([qa[b, at, h] for h in heads], axis=0)
            gn = jnp.concatenate([ga[b, at, h] for h in heads], axis=0)
            return qn, gn

        def products(i):
            qn, gn = operands(i)
            return [(dot(kv[s, 0], qn, ((1,), (1,))), dot(kv[s, 1], gn, ((1,), (1,)))) for s in slots]

        def weights(i, out):
            b, u = units[i]
            norm, delta = st[b, u:u + 1, :], st[b, u + 4:u + 5, :]
            query_block = (x * NZ + z) * NY + b
            query_len = count_ref[query_block] * UNIT
            row_in = u * UNIT + lane
            for j, (scores, dp) in enumerate(out):
                key_block = slots[j] * NY + y
                key_len = count_ref[key_block] * UNIT
                most = jnp.where(query_block > key_block, CAP, -1)
                limit = jnp.where(query_block == key_block, row_in, most)
                limit = jnp.where(row_in < query_len, jnp.minimum(limit, key_len - 1), -1)
                prob = jnp.exp2(scores * (SCALE * LOG2E) - norm)
                prob = jnp.where(key <= limit, prob, 0.0)
                db[i % 2, j] = (prob * (dp - delta)).astype(BF16)
                pb[i % 2, j] = prob.astype(BF16)

        def grads(i):
            qn, gn = operands(i)
            for j, slot in enumerate(slots):
                for p, (left, right) in enumerate(((db, qn), (pb, gn))):
                    total = dot(left[i % 2, j], right, ((1,), (0,)))
                    acc[slot, p] = total if fresh and i == 0 else acc[slot, p] + total
            b, u = units[i]
            total = dot(kt[slots[0]], db[i % 2, 0], ((1,), (0,)))
            for j in range(1, len(slots)):
                total = total + dot(kt[slots[j]], db[i % 2, j], ((1,), (0,)))
            dqt[b, u] += total

        weights(0, products(0))
        for i in range(1, len(units)):
            out = products(i)
            grads(i - 1)
            weights(i, out)
        grads(len(units) - 1)

    def pair(row, g):
        if isinstance(g, int):
            return [(row, g), (row, -g if g else 4)]
        return [(row, g), (row, 4 * (1 - (g + 3) // 4) - g)]

    for s in range(1, 3):
        for d in range(2):
            for p in range(2):
                ring(d, p, s - 1).wait_recv()
                ring(d, p, s).start()
                if s == 1:
                    @pl.when(x == 0)
                    def _():
                        cross(CROSS.index(-DIRS[d]), p).start()
        if s == 2:
            side(0, 0).wait_recv()
            far_side(0, 0).start()
            side(0, 2).wait_recv()
            far_side(0, 2).start()
        block(pair(x, s), [y], True)

    @pl.when(x == 1)
    def _():
        for d in range(2):
            for p in range(2):
                crossed(CROSS.index(-DIRS[d]), p).wait_recv()
                extra(d, p, 1).start()

    for d in range(2):
        for p in range(2):
            ring(d, p, 2).wait_recv()
            if valid(d, p, 3):
                ring(d, p, 3).start()
    side(1, 1).wait_recv()
    far_side(1, 1).start()
    block(pair(x, 3), [y], True)

    @pl.when(x == 1)
    def _():
        for d in range(2):
            for p in range(2):
                extra(d, p, 1).wait_recv()
                extra(d, p, 2).start()
        block(pair(0, 1), [y], True)

    for p in range(2):
        ring(p, p, 3).wait_recv()
    block(pair(x, 0), [y], True)

    @pl.when(x == 1)
    def _():
        for d in range(2):
            for p in range(2):
                extra(d, p, 2).wait_recv()
                if valid(d, p, 3):
                    extra(d, p, 3).start()
        for p in range(2):
            crossed(0, p).wait_recv()

        @pl.loop(2, 4)
        def _(g):
            block(pair(0, g), [y], True)

    side(1, 0).wait_recv()
    side(0, 1).wait_recv()
    side(1, 2).wait_recv()
    for d, a in ((0, 0), (1, 1), (0, 2)):
        far_side(d, a).wait_recv()

    copies = weight_copies((wq, wk, wv), wbuf, wsem, 0)

    @pl.when(x == 1)
    def _():
        for p in range(2):
            extra(p, p, 3).wait_recv()
        block(pair(0, 0), [y], True)

    @pl.loop(0, 4 * (1 + x))
    def _(t):
        block(pair(x * (1 - t // 4), lax.rem(t, 4)), [yy(2)], False)

    tall = fst.shape[0]
    parts = (slice(0, tall // 2), slice(tall // 2, tall))

    def far_grad(d):
        return move(fst.at[parts[d]], frb.at[parts[d]], sy.at[0, 0, d], sy.at[0, 1, d], along_y(d))

    def side_grad(d):
        return move(yst.at[d], yrb.at[d], sy.at[1, 0, d], sy.at[1, 1, d], along_y(d))

    def query_grad(b):
        return jnp.concatenate([dqt[b, u] * SCALE for u in range(UNITS)], axis=0)

    fst[...] = query_grad(yy(2)).astype(BF16)
    for d in range(2):
        far_grad(d).start()

    def sum_ring(d, p, s):
        return move(zst.at[d, p, s], zrb.at[d, p, s], sz.at[0, 0, d, p, s], sz.at[0, 1, d, p, s], along_z(d))

    def sum_extra(d, p, s):
        return move(est.at[d, p, s], erb.at[d, p, s], sz.at[1, 0, d, p, s], sz.at[1, 1, d, p, s], along_z(d))

    def sum_cross(i, p):
        return move(xst.at[i, p], xrb.at[i, p], sx.at[0, i, p], sx.at[1, i, p], twin)

    def term(row, e, p):
        value = acc[row * NZ + zz(e), p]
        return value * SCALE if p == 0 else value

    def starts(d, p, s):
        return s > 0 or d == p

    def both_ways(row, level):
        ends = (level,) if level in (0, 4) else (level, -level)
        block([(row, e) for e in ends], [yy(1), yy(-1)], False)

    for s in range(4):
        far_off = 4 - s

        @pl.when(x == 1)
        def _():
            both_ways(0, far_off)
            for d in range(2):
                for p in range(2):
                    e = DIRS[d] * far_off
                    if not starts(d, p, s):
                        continue
                    value = term(0, e, p)
                    if s in (1, 2) and starts(d, p, s - 1):
                        sum_extra(d, p, s - 1).wait_recv()
                        value = value + erb[d, p, s - 1].astype(F32)
                    if s < 2:
                        est[d, p, s] = value.astype(BF16)
                        sum_extra(d, p, s).start()
                    else:
                        xst[CROSS.index(e), p] = value.astype(BF16)
                        sum_cross(CROSS.index(e), p).start()

        both_ways(x, far_off)
        for d in range(2):
            for p in range(2):
                if not starts(d, p, s):
                    continue
                value = term(x, DIRS[d] * far_off, p)
                if s > 0 and starts(d, p, s - 1):
                    sum_ring(d, p, s - 1).wait_recv()
                    value = value + zrb[d, p, s - 1].astype(F32)
                zst[d, p, s] = value.astype(BF16)
                if s >= 2:
                    @pl.when(x == 0)
                    def _():
                        i = CROSS.index(DIRS[d] * far_off)
                        sum_cross(i, p).wait_recv()
                        zst[d, p, s] = (value + xrb[i, p].astype(F32)).astype(BF16)
                sum_ring(d, p, s).start()

    @pl.when(x == 1)
    def _():
        both_ways(0, 0)
        for p in range(2):
            xst[0, p] = term(0, 0, p).astype(BF16)
            sum_cross(0, p).start()

    both_ways(x, 0)
    for d in range(2):
        far_grad(d).wait_recv()
        value = query_grad(yy(DIRS[d]))
        yst[d] = value.astype(BF16)
        yst[d, parts[d]] = (value[parts[d]] + frb[parts[d]].astype(F32)).astype(BF16)
        side_grad(d).start()
    for group in copies:
        for copy in group:
            copy.wait()

    outs = (dk_out, dv_out)
    row_of = lax.broadcasted_iota(jnp.int32, (CAP, HD), 0)
    for p in range(2):
        value = term(x, 0, p)
        for d in range(2):
            sum_ring(d, p, 3).wait_recv()
            value = value + zrb[d, p, 3].astype(F32)
        outs[p][...] = value

        @pl.when(x == 0)
        def _():
            sum_cross(0, p).wait_recv()
            outs[p][...] = value + xrb[0, p].astype(F32)

        act[:, (GROUP + p) * HD:(GROUP + p + 1) * HD] = outs[p][...].astype(BF16)

    value = query_grad(y)
    for d in range(2):
        side_grad(d).wait_recv()
        value = value + yrb[d].astype(F32)
    for u in range(UNITS):
        turned = value[u * HD:(u + 1) * HD].T.astype(BF16)
        for h in range(GROUP):
            act[u * UNIT:(u + 1) * UNIT, h * HD:(h + 1) * HD] = turned[h * UNIT:(h + 1) * UNIT]

    def columns(c):
        return pl.ds(pl.multiple_of(c * width, width), width)

    height = CAP // PIECES
    rows = [pl.ds(i * height, height) for i in range(PIECES)]

    def swap(i, which):
        src, dst = ((far, farb), (near, nearb))[which]
        return move(
            src.at[rows[i], columns(1 - core)], dst.at[rows[i]], hs.at[which, 0, i], hs.at[which, 1, i], partner
        )

    def hop(i):
        return move(stage.at[rows[i]], relay.at[rows[i]], hs.at[2, 0, i], hs.at[2, 1, i], device(DIRS[i % 2]))

    def forward(i):
        return move(relay.at[rows[i]], last.at[rows[i]], hs.at[3, 0, i], hs.at[3, 1, i], device(DIRS[i % 2]))

    def product(c):
        return dot(act[...], wbuf[c], ((1,), (1,))).astype(BF16)

    for c in range(tiles):
        far[:, c * TILE:(c + 1) * TILE] = product((1 - x_hi) * tiles + c)
    for i in range(PIECES):
        swap(i, 0).start()
    for i in range(PIECES):
        swap(i, 0).wait_recv()
        mine = far[rows[i], columns(core)].astype(F32)
        stage[rows[i]] = (mine + farb[rows[i]].astype(F32)).astype(BF16)
        hop(i).start()
    for c in range(tiles):
        near[:, c * TILE:(c + 1) * TILE] = product(x_hi * tiles + c)
    for i in range(PIECES):
        swap(i, 1).start()
    for i in range(PIECES):
        hop(i).wait_recv()
        forward(i).start()
    for i in range(PIECES):
        swap(i, 1).wait_recv()
        forward(i).wait_recv()
        mine = near[rows[i], columns(core)].astype(F32)
        total = mine + nearb[rows[i]].astype(F32) + last[rows[i]].astype(F32)
        out_ref[rows[i]] = total.astype(BF16)

    for d in range(2):
        for p in range(2):
            for s in range(4):
                if valid(d, p, s):
                    ring(d, p, s).wait_send()
                if starts(d, p, s):
                    sum_ring(d, p, s).wait_send()
        for a in range(3):
            side(d, a).wait_send()
        far_grad(d).wait_send()
        side_grad(d).wait_send()
    for d, a in ((0, 0), (1, 1), (0, 2)):
        far_side(d, a).wait_send()

    @pl.when(x == 0)
    def _():
        for p in range(2):
            for i in range(3):
                cross(i, p).wait_send()

    @pl.when(x == 1)
    def _():
        for p in range(2):
            for d in range(2):
                for s in range(1, 4):
                    if valid(d, p, s):
                        extra(d, p, s).wait_send()
                for s in range(2):
                    if starts(d, p, s):
                        sum_extra(d, p, s).wait_send()
            for i in range(5):
                sum_cross(i, p).wait_send()

    for i in range(PIECES):
        for which in range(2):
            swap(i, which).wait_send()
        hop(i).wait_send()
        forward(i).wait_send()


def on_device(q, k, v, o, g, lse, counts, wq, wk, wv):
    dma = pltpu.SemaphoreType.DMA
    hbm = pl.BlockSpec(memory_space=pl.ANY)
    blocks, units = NX * NZ, CAP // UNIT
    model = wq.shape[0]
    features = wq.shape[1] + wk.shape[1] + wv.shape[1]
    tile = (CAP, HD)
    flat = (units * HD, GROUP * UNIT)
    quarter = (CAP, model // 4)

    def vmem(shape, dtype=BF16):
        return pltpu.VMEM(shape, dtype)

    return pl.pallas_call(
        fused_kernel,
        name="attention_backward",
        out_shape=(
            jax.ShapeDtypeStruct(quarter, BF16),
            jax.ShapeDtypeStruct(tile, F32),
            jax.ShapeDtypeStruct(tile, F32),
        ),
        in_specs=[SMEM] + [VMEM] * 6 + [hbm] * 3,
        out_specs=(VMEM,) * 3,
        scratch_shapes=[
            vmem((blocks, 2) + tile),
            vmem((NY, CAP, GROUP * HD)),
            vmem((NY, CAP, GROUP * HD)),
            vmem((NY, 8, GROUP * UNIT), F32),
            vmem((blocks, HD, CAP)),
            vmem((blocks, 2) + tile, F32),
            vmem((NY, units, HD, GROUP * UNIT), F32),
            vmem((2, 2, CAP, GROUP * UNIT)), vmem((2, 2, CAP, GROUP * UNIT)),
            vmem((2, 2, 4) + tile), vmem((2, 2, 4) + tile),
            vmem((2, 2, 2) + tile), vmem((2, 2, 2) + tile),
            vmem((5, 2) + tile), vmem((5, 2) + tile),
            vmem(flat), vmem(flat), vmem((2,) + flat), vmem((2,) + flat),
            vmem((CAP, features)),
            vmem((CAP, model // 2)), vmem((CAP, model // 2)),
            vmem(quarter), vmem(quarter), vmem(quarter), vmem(quarter), vmem(quarter),
            vmem((model // TILE, TILE, features)),
            dma((2, 2, 2, 2, 4)), dma((2, 3, 2)), dma((2, 2, 2, 3)),
            dma((2, 2, 2, 2, 4)), dma((2, 5, 2)), dma((2, 2, 2)),
            dma((4, 2, PIECES)), dma((model // TILE, 3)),
        ],
        compiler_params=pltpu.CompilerParams(collective_id=0, has_side_effects=True),
    )(counts, k, v, q, g, o, lse, wq, wk, wv)


def solution(mesh):
    return jax.shard_map(
        on_device,
        mesh=mesh,
        in_specs=(
            P("ctx", "heads"), P("ctx", "heads"), P("ctx", "heads"), P("ctx", "heads"), P("ctx", "heads"),
            P("heads", "ctx"), P(), P(None, "heads"), P(None, "heads"), P(None, "heads"),
        ),
        out_specs=(P("ctx", "heads"), P("ctx", "heads"), P("ctx", "heads")),
        check_vma=False,
    )
```

time: 948 us -> 87.8 us (0.09)
  waiting for transfers between devices: 690 us -> 0 us
  matrix products: 201 us -> 0 us
  Pallas kernels: 0 us -> 82.1 us
  other arithmetic: 24.3 us -> 0 us
  between operations: 13.9 us -> 0.64 us
  local copies, waits for them, and re-layouts: 14.7 us -> 4.84 us
    reduce_scatter x2 -> x0, waiting for transfers between devices: 427 us -> none  [the longest x1 336 us: in_one_piece_2(): lax.psum_scatter(both, axis, scatter_dimension=dim, tiled=True)]
    all_gather x1 -> x0, waiting for transfers between devices: 262 us -> none  [in_one_piece(): result = lax.all_gather(both, axis, axis=dim, tiled=True)]
    dot_general x163 -> x0, matrix products: 201 us -> none  [the longest x32 42.7 us: tile_grads(): jnp.einsum('qgd,kd->gqk', query_blk, key_blk, preferred_element_type=jnp....]
    pallas_call x0 -> x1, Pallas kernels: none -> 82.1 us  [on_device(): pl.pallas_call(fused_kernel, name='attention_backward', out_shape=(jax.Sh...]
    concatenate x2 -> x0, other arithmetic: 11.6 us -> none  [the longest x1 10.1 us: in_one_piece_2(): both = jnp.concatenate(arrays, axis=along)]
  transfers between devices with their start and end apart: 3 -> 0, of which waited for: 3 -> 0; matrix products, arithmetic and copies ran while one was open for 1% -> 0% of each run, Pallas kernels for 0% -> 0%
where the time goes in v2:
time: 87.8 us; the launch traced here: 87.6 us
  Pallas kernels  82.1 us (94%)
  local copies, waits for them, and re-layouts  4.84 us (6%)
    pallas_call x1, Pallas kernels, on_device(): pl.pallas_call(fused_kernel, name='attention_backward', out_shape=(jax.Sh...  82.1 us
    unnamed x3, local copies, waits for them, and re-layouts  4.84 us

profile of v2, /device:TPU:1, one launch (start us, length us, event | category | flops | bytes accessed | tf_op | source)
XLA Modules:
  0.0 87.6 jit_solution(5056859034689334181)
XLA Ops:
  0.6 82.1 %attention_backward.1 = (bf16[192,1024]{1,0:T(8,128)(2,1)}, f32[192,128]{1,0:T(8,128)}, f32[192,128]{1,0:T(8,128)}) custom-call(s32[64]{0:T(128)} %count_ref.1, bf16[192,128]{1,0:T(8,128)(2,1)} %k_ref.1, bf16[192,128]{1,0:T(8,128)(2,1)} %v_ref.1, bf16[192,512]{1,0:T(8,128)(2,1)} %q_ref.1, bf16[192,512]{1,0:T(8,128)(2,1)} %g_ref.1, bf16[192,512]{1,0:T(8,128)(2,1)} %o_ref.1, ...), custom_call_target="tpu_custom_call" | custom-call | tf_op jit(solution)/shard_map/attention_backward/pallas_call | solution.py:528
  82.7 1.8 %copy.16 = bf16[192,1024]{1,0:T(8,128)(2,1)} copy(bf16[192,1024]{1,0:T(8,128)(2,1)} %get-tuple-element.6) | data formatting | bytes 786432
  84.5 1.5 %copy.17 = f32[192,128]{1,0:T(8,128)} copy(f32[192,128]{1,0:T(8,128)} %get-tuple-element.7) | data formatting | bytes 196608
  86.0 1.5 %copy.18 = f32[192,128]{1,0:T(8,128)} copy(f32[192,128]{1,0:T(8,128)} %get-tuple-element.8) | data formatting | bytes 196608

commit v3 on v2

--- a/solution.py
+++ b/solution.py
@@ -46,7 +46,7 @@
 
 
 DIRS = (1, -1)
-CROSS = (0, 1, -1, 2, -2)
+CROSS = (0, 1, -1)
 
 
 def weight_copies(w_refs, buf, sems, first):
@@ -104,57 +104,6 @@
         return ctx_id(x, z, yy(DIRS[d]))
 
     twin = ctx_id(1 - x, z, y)
-    greet([along_z(0), along_z(1), along_y(0), along_y(1), partner, device(1), device(-1)])
-
-    def ring(d, p, s):
-        slot = x * NZ + zz(-DIRS[d] * s)
-        src = own[p] if s == 0 else kv.at[slot, p]
-        return move(src, kv.at[slot, p], gz.at[0, 0, d, p, s], gz.at[0, 1, d, p, s], along_z(d))
-
-    def extra(d, p, s):
-        slot = zz(-DIRS[d] * s)
-        return move(kv.at[slot, p], kv.at[slot, p], gz.at[1, 0, d, p, s], gz.at[1, 1, d, p, s], along_z(d))
-
-    def cross(i, p):
-        slot = zz(CROSS[i])
-        src = own[p] if i == 0 else kv.at[slot, p]
-        return move(src, kv.at[slot, p], gx.at[0, i, p], gx.at[1, i, p], twin)
-
-    def crossed(i, p):
-        slot = zz(CROSS[i])
-        return move(kv.at[slot, p], kv.at[slot, p], gx.at[0, i, p], gx.at[1, i, p], twin)
-
-    sources, targets = (q_ref, g_ref, st.at[y]), (qa, ga, st)
-
-    def side(d, a):
-        return move(sources[a], targets[a].at[y], gy.at[0, 0, d, a], gy.at[0, 1, d, a], along_y(d))
-
-    def far_side(d, a):
-        slot = yy(-DIRS[d])
-        return move(
-            targets[a].at[slot], targets[a].at[slot], gy.at[1, 0, d, a], gy.at[1, 1, d, a], along_y(d)
-        )
-
-    def valid(d, p, s):
-        return s < 3 or d == p
-
-    for p in range(2):
-        for d in range(2):
-            ring(d, p, 0).start()
-
-    @pl.when(x == 0)
-    def _():
-        for p in range(2):
-            cross(0, p).start()
-
-    side(0, 0).start()
-    side(1, 1).start()
-    side(1, 0).start()
-    side(0, 1).start()
-    kv[x * NZ + z, 0] = k_ref[...]
-    kv[x * NZ + z, 1] = v_ref[...]
-    qa[y] = q_ref[...]
-    ga[y] = g_ref[...]
     st[y] = jnp.zeros(st.shape[1:], F32)
     for h in range(GROUP):
         cols = slice(h * HD, (h + 1) * HD)
@@ -166,8 +115,59 @@
             into = slice(h * UNIT, (h + 1) * UNIT)
             st[y, u:u + 1, into] = norm[:, part]
             st[y, u + 4:u + 5, into] = delta[:, part]
+    greet([along_z(0), along_z(1), along_y(0), along_y(1), partner, device(1), device(-1)])
+
+    def ring(d, p, s):
+        slot = x * NZ + zz(-DIRS[d] * s)
+        src = own[p] if s == 0 else kv.at[slot, p]
+        return move(src, kv.at[slot, p], gz.at[0, 0, d, p, s], gz.at[0, 1, d, p, s], along_z(d))
+
+    def extra(d, p, s):
+        slot = zz(-DIRS[d] * s)
+        return move(kv.at[slot, p], kv.at[slot, p], gz.at[1, 0, d, p, s], gz.at[1, 1, d, p, s], along_z(d))
+
+    def cross(i, p):
+        slot = zz(CROSS[i])
+        src = own[p] if i == 0 else kv.at[slot, p]
+        return move(src, kv.at[slot, p], gx.at[0, i, p], gx.at[1, i, p], twin)
+
+    def crossed(i, p):
+        slot = zz(CROSS[i])
+        return move(kv.at[slot, p], kv.at[slot, p], gx.at[0, i, p], gx.at[1, i, p], twin)
+
+    sources, targets = (q_ref, g_ref, st.at[y]), (qa, ga, st)
+
+    def side(d, a):
+        return move(sources[a], targets[a].at[y], gy.at[0, 0, d, a], gy.at[0, 1, d, a], along_y(d))
+
+    def far_side(d, a):
+        slot = yy(-DIRS[d])
+        return move(
+            targets[a].at[slot], targets[a].at[slot], gy.at[1, 0, d, a], gy.at[1, 1, d, a], along_y(d)
+        )
+
+    def valid(d, p, s):
+        return s < 3 or d == p
+
+    for p in range(2):
+        for d in range(2):
+            ring(d, p, 0).start()
+
+    @pl.when(x == 0)
+    def _():
+        for p in range(2):
+            cross(0, p).start()
+
     side(0, 2).start()
     side(1, 2).start()
+    side(0, 0).start()
+    side(1, 1).start()
+    side(1, 0).start()
+    side(0, 1).start()
+    kv[x * NZ + z, 0] = k_ref[...]
+    kv[x * NZ + z, 1] = v_ref[...]
+    qa[y] = q_ref[...]
+    ga[y] = g_ref[...]
     dqt[...] = jnp.zeros_like(dqt)
 
     lane = lax.rem(lax.broadcasted_iota(jnp.int32, (1, GROUP * UNIT), 1), UNIT)
@@ -234,8 +234,8 @@
         return [(row, g), (row, 4 * (1 - (g + 3) // 4) - g)]
 
     for s in range(1, 3):
-        for d in range(2):
-            for p in range(2):
+        for p in range(2):
+            for d in range(2):
                 ring(d, p, s - 1).wait_recv()
                 ring(d, p, s).start()
                 if s == 1:
@@ -251,13 +251,13 @@
 
     @pl.when(x == 1)
     def _():
-        for d in range(2):
-            for p in range(2):
+        for p in range(2):
+            for d in range(2):
                 crossed(CROSS.index(-DIRS[d]), p).wait_recv()
                 extra(d, p, 1).start()
 
-    for d in range(2):
-        for p in range(2):
+    for p in range(2):
+        for d in range(2):
             ring(d, p, 2).wait_recv()
             if valid(d, p, 3):
                 ring(d, p, 3).start()
@@ -267,10 +267,18 @@
 
     @pl.when(x == 1)
     def _():
-        for d in range(2):
-            for p in range(2):
+        for p in range(2):
+            for d in range(2):
                 extra(d, p, 1).wait_recv()
                 extra(d, p, 2).start()
+
+    side(1, 0).wait_recv()
+    side(0, 1).wait_recv()
+    side(1, 2).wait_recv()
+    block(pair(x, 1), [yy(1), yy(-1)], False)
+
+    @pl.when(x == 1)
+    def _():
         block(pair(0, 1), [y], True)
 
     for p in range(2):
@@ -279,8 +287,8 @@
 
     @pl.when(x == 1)
     def _():
-        for d in range(2):
-            for p in range(2):
+        for p in range(2):
+            for d in range(2):
                 extra(d, p, 2).wait_recv()
                 if valid(d, p, 3):
                     extra(d, p, 3).start()
@@ -291,9 +299,7 @@
         def _(g):
             block(pair(0, g), [y], True)
 
-    side(1, 0).wait_recv()
-    side(0, 1).wait_recv()
-    side(1, 2).wait_recv()
+    block([(x, 0)], [yy(1), yy(-1)], False)
     for d, a in ((0, 0), (1, 1), (0, 2)):
         far_side(d, a).wait_recv()
 
@@ -305,10 +311,6 @@
             extra(p, p, 3).wait_recv()
         block(pair(0, 0), [y], True)
 
-    @pl.loop(0, 4 * (1 + x))
-    def _(t):
-        block(pair(x * (1 - t // 4), lax.rem(t, 4)), [yy(2)], False)
-
     tall = fst.shape[0]
     parts = (slice(0, tall // 2), slice(tall // 2, tall))
 
@@ -320,85 +322,123 @@
 
     def query_grad(b):
         return jnp.concatenate([dqt[b, u] * SCALE for u in range(UNITS)], axis=0)
+
+    def sum_ring(d, p, s):
+        return move(zst.at[d, p, s], zrb.at[d, p, s], sz.at[0, 0, d, p, s], sz.at[0, 1, d, p, s], along_z(d))
+
+    def sum_extra(d, p, s):
+        return move(est.at[d, p, s], erb.at[d, p, s], sz.at[1, 0, d, p, s], sz.at[1, 1, d, p, s], along_z(d))
+
+    def sum_cross(i, p):
+        return move(xst.at[i, p], xrb.at[i, p], sx.at[0, i, p], sx.at[1, i, p], twin)
+
+    def term(row, e, p):
+        value = acc[row * NZ + zz(e), p]
+        return value * SCALE if p == 0 else value
+
+    def starts(d, p, s):
+        return s > 0 or s == 0 and d == p
+
+    def rest(row, level, shifts):
+        ends = (level,) if level in (0, 4) else (level, -level)
+        block([(row, e) for e in ends], [yy(k) for k in shifts], False)
+
+    sides, three = (1, -1), (2, 1, -1)
+
+    def send_first_row(s):
+        for p in range(2):
+            for d in range(2):
+                if not starts(d, p, s):
+                    continue
+                value = term(0, DIRS[d] * (4 - s), p)
+                if starts(d, p, s - 1):
+                    sum_extra(d, p, s - 1).wait_recv()
+                    value = value + erb[d, p, s - 1].astype(F32)
+                if s < 3:
+                    est[d, p, s] = value.astype(BF16)
+                    sum_extra(d, p, s).start()
+                else:
+                    xst[CROSS.index(DIRS[d]), p] = value.astype(BF16)
+                    sum_cross(CROSS.index(DIRS[d]), p).start()
+
+    def send_own_row(s):
+        for p in range(2):
+            for d in range(2):
+                if not starts(d, p, s):
+                    continue
+                value = term(x, DIRS[d] * (4 - s), p)
+                if starts(d, p, s - 1):
+                    sum_ring(d, p, s - 1).wait_recv()
+                    value = value + zrb[d, p, s - 1].astype(F32)
+                zst[d, p, s] = value.astype(BF16)
+                if s == 3:
+                    @pl.when(x == 0)
+                    def _():
+                        i = CROSS.index(DIRS[d])
+                        sum_cross(i, p).wait_recv()
+                        zst[d, p, s] = (value + xrb[i, p].astype(F32)).astype(BF16)
+                sum_ring(d, p, s).start()
+
+    @pl.when(x == 1)
+    def _():
+        rest(0, 4, three)
+        send_first_row(0)
+
+    rest(x, 4, three)
+    send_own_row(0)
+
+    @pl.when(x == 1)
+    def _():
+        rest(0, 3, three)
+        send_first_row(1)
+
+    @pl.loop(0, 2 + x)
+    def _(t):
+        block(pair(x * (1 - t // 2), 1 + lax.rem(t, 2)), [yy(2)], False)
+
+    rest(x, 3, three)
+    send_own_row(1)
+
+    @pl.when(x == 1)
+    def _():
+        rest(0, 2, three)
+        send_first_row(2)
+        block([(0, 0), (1, 0)], [yy(2)], False)
+
+    @pl.when(x == 0)
+    def _():
+        rest(0, 0, (2,))
 
     fst[...] = query_grad(yy(2)).astype(BF16)
     for d in range(2):
         far_grad(d).start()
 
-    def sum_ring(d, p, s):
-        return move(zst.at[d, p, s], zrb.at[d, p, s], sz.at[0, 0, d, p, s], sz.at[0, 1, d, p, s], along_z(d))
-
-    def sum_extra(d, p, s):
-        return move(est.at[d, p, s], erb.at[d, p, s], sz.at[1, 0, d, p, s], sz.at[1, 1, d, p, s], along_z(d))
-
-    def sum_cross(i, p):
-        return move(xst.at[i, p], xrb.at[i, p], sx.at[0, i, p], sx.at[1, i, p], twin)
-
-    def term(row, e, p):
-        value = acc[row * NZ + zz(e), p]
-        return value * SCALE if p == 0 else value
-
-    def starts(d, p, s):
-        return s > 0 or d == p
-
-    def both_ways(row, level):
-        ends = (level,) if level in (0, 4) else (level, -level)
-        block([(row, e) for e in ends], [yy(1), yy(-1)], False)
-
-    for s in range(4):
-        far_off = 4 - s
-
-        @pl.when(x == 1)
-        def _():
-            both_ways(0, far_off)
-            for d in range(2):
-                for p in range(2):
-                    e = DIRS[d] * far_off
-                    if not starts(d, p, s):
-                        continue
-                    value = term(0, e, p)
-                    if s in (1, 2) and starts(d, p, s - 1):
-                        sum_extra(d, p, s - 1).wait_recv()
-                        value = value + erb[d, p, s - 1].astype(F32)
-                    if s < 2:
-                        est[d, p, s] = value.astype(BF16)
-                        sum_extra(d, p, s).start()
-                    else:
-                        xst[CROSS.index(e), p] = value.astype(BF16)
-                        sum_cross(CROSS.index(e), p).start()
-
-        both_ways(x, far_off)
-        for d in range(2):
-            for p in range(2):
-                if not starts(d, p, s):
-                    continue
-                value = term(x, DIRS[d] * far_off, p)
-                if s > 0 and starts(d, p, s - 1):
-                    sum_ring(d, p, s - 1).wait_recv()
-                    value = value + zrb[d, p, s - 1].astype(F32)
-                zst[d, p, s] = value.astype(BF16)
-                if s >= 2:
-                    @pl.when(x == 0)
-                    def _():
-                        i = CROSS.index(DIRS[d] * far_off)
-                        sum_cross(i, p).wait_recv()
-                        zst[d, p, s] = (value + xrb[i, p].astype(F32)).astype(BF16)
-                sum_ring(d, p, s).start()
-
-    @pl.when(x == 1)
-    def _():
-        both_ways(0, 0)
+    @pl.when(x == 1)
+    def _():
+        rest(0, 1, sides)
+
+    rest(x, 2, sides)
+
+    @pl.when(x == 1)
+    def _():
+        send_first_row(3)
+
+    send_own_row(2)
+
+    @pl.when(x == 1)
+    def _():
+        rest(0, 0, sides)
         for p in range(2):
             xst[0, p] = term(0, 0, p).astype(BF16)
             sum_cross(0, p).start()
 
-    both_ways(x, 0)
     for d in range(2):
         far_grad(d).wait_recv()
         value = query_grad(yy(DIRS[d]))
         yst[d] = value.astype(BF16)
         yst[d, parts[d]] = (value[parts[d]] + frb[parts[d]].astype(F32)).astype(BF16)
         side_grad(d).start()
+    send_own_row(3)
     for group in copies:
         for copy in group:
             copy.wait()
@@ -499,10 +539,10 @@
                 for s in range(1, 4):
                     if valid(d, p, s):
                         extra(d, p, s).wait_send()
-                for s in range(2):
+                for s in range(3):
                     if starts(d, p, s):
                         sum_extra(d, p, s).wait_send()
-            for i in range(5):
+            for i in range(3):
                 sum_cross(i, p).wait_send()
 
     for i in range(PIECES):
@@ -510,6 +550,11 @@
             swap(i, which).wait_send()
         hop(i).wait_send()
         forward(i).wait_send()
+
+
+def hand_over(*refs):
+    for i in range(3):
+        refs[i + 3][...] = refs[i][...]
 
 
 def on_device(q, k, v, o, g, lse, counts, wq, wk, wv):
@@ -525,7 +570,7 @@
     def vmem(shape, dtype=BF16):
         return pltpu.VMEM(shape, dtype)
 
-    return pl.pallas_call(
+    outs = pl.pallas_call(
         fused_kernel,
         name="attention_backward",
         out_shape=(
@@ -545,19 +590,26 @@
             vmem((NY, units, HD, GROUP * UNIT), F32),
             vmem((2, 2, CAP, GROUP * UNIT)), vmem((2, 2, CAP, GROUP * UNIT)),
             vmem((2, 2, 4) + tile), vmem((2, 2, 4) + tile),
-            vmem((2, 2, 2) + tile), vmem((2, 2, 2) + tile),
-            vmem((5, 2) + tile), vmem((5, 2) + tile),
+            vmem((2, 2, 3) + tile), vmem((2, 2, 3) + tile),
+            vmem((3, 2) + tile), vmem((3, 2) + tile),
             vmem(flat), vmem(flat), vmem((2,) + flat), vmem((2,) + flat),
             vmem((CAP, features)),
             vmem((CAP, model // 2)), vmem((CAP, model // 2)),
             vmem(quarter), vmem(quarter), vmem(quarter), vmem(quarter), vmem(quarter),
             vmem((model // TILE, TILE, features)),
             dma((2, 2, 2, 2, 4)), dma((2, 3, 2)), dma((2, 2, 2, 3)),
-            dma((2, 2, 2, 2, 4)), dma((2, 5, 2)), dma((2, 2, 2)),
+            dma((2, 2, 2, 2, 4)), dma((2, 3, 2)), dma((2, 2, 2)),
             dma((4, 2, PIECES)), dma((model // TILE, 3)),
         ],
         compiler_params=pltpu.CompilerParams(collective_id=0, has_side_effects=True),
     )(counts, k, v, q, g, o, lse, wq, wk, wv)
+    return pl.pallas_call(
+        hand_over,
+        name="hand_over",
+        out_shape=tuple(jax.ShapeDtypeStruct(a.shape, a.dtype) for a in outs),
+        in_specs=[VMEM] * 3,
+        out_specs=(VMEM,) * 3,
+    )(*outs)
 
 
 def solution(mesh):

time: 87.8 us -> 77.8 us (0.89)
  Pallas kernels: 82.1 us -> 77 us
  local copies, waits for them, and re-layouts: 4.84 us -> 0 us
    pallas_call x1, Pallas kernels: 82.1 us -> 75.1 us  [on_device(): pl.pallas_call(fused_kernel, name='attention_backward', out_shape=(jax.Sh...]
    unnamed x3 -> x0, local copies, waits for them, and re-layouts: 4.84 us -> none
    pallas_call x0 -> x1, Pallas kernels: none -> 1.87 us  [on_device(): pl.pallas_call(hand_over, name='hand_over', out_shape=tuple((jax.ShapeDty...]
where the time goes in v3:
time: 77.8 us; the launch traced here: 77.6 us
  Pallas kernels  77 us (99%)
    pallas_call x1, Pallas kernels, on_device(): pl.pallas_call(fused_kernel, name='attention_backward', out_shape=(jax.Sh...  75.1 us
    pallas_call x1, Pallas kernels, on_device(): pl.pallas_call(hand_over, name='hand_over', out_shape=tuple((jax.ShapeDty...  1.87 us

profile of v3, /device:TPU:1, one launch (start us, length us, event | category | flops | bytes accessed | tf_op | source)
XLA Modules:
  0.0 77.6 jit_solution(11254537591717490750)
XLA Ops:
  0.6 75.1 %attention_backward.1 = (bf16[192,1024]{1,0:T(8,128)(2,1)}, f32[192,128]{1,0:T(8,128)}, f32[192,128]{1,0:T(8,128)}) custom-call(s32[64]{0:T(128)} %count_ref.1, bf16[192,128]{1,0:T(8,128)(2,1)} %k_ref.1, bf16[192,128]{1,0:T(8,128)(2,1)} %v_ref.1, bf16[192,512]{1,0:T(8,128)(2,1)} %q_ref.1, bf16[192,512]{1,0:T(8,128)(2,1)} %g_ref.1, bf16[192,512]{1,0:T(8,128)(2,1)} %o_ref.1, ...), custom_call_target="tpu_custom_call" | custom-call | tf_op jit(solution)/shard_map/attention_backward/pallas_call | solution.py:573
  75.8 1.9 %hand_over.1 = (bf16[192,1024]{1,0:T(8,128)(2,1)}, f32[192,128]{1,0:T(8,128)}, f32[192,128]{1,0:T(8,128)}) custom-call(bf16[192,1024]{1,0:T(8,128)(2,1)} %get-tuple-element.6.refs_0_, f32[192,128]{1,0:T(8,128)} %get-tuple-element.7.refs_1_, f32[192,128]{1,0:T(8,128)} %get-tuple-element.8.refs_2_), custom_call_target="tpu_custom_call" | custom-call | tf_op jit(solution)/shard_map/hand_over/pallas_call | solution.py:606

commit v4 on v3

--- a/solution.py
+++ b/solution.py
@@ -242,11 +242,6 @@
                     @pl.when(x == 0)
                     def _():
                         cross(CROSS.index(-DIRS[d]), p).start()
-        if s == 2:
-            side(0, 0).wait_recv()
-            far_side(0, 0).start()
-            side(0, 2).wait_recv()
-            far_side(0, 2).start()
         block(pair(x, s), [y], True)
 
     @pl.when(x == 1)
@@ -256,6 +251,10 @@
                 crossed(CROSS.index(-DIRS[d]), p).wait_recv()
                 extra(d, p, 1).start()
 
+    side(0, 0).wait_recv()
+    far_side(0, 0).start()
+    side(0, 2).wait_recv()
+    far_side(0, 2).start()
     for p in range(2):
         for d in range(2):
             ring(d, p, 2).wait_recv()
@@ -396,13 +395,16 @@
     def _(t):
         block(pair(x * (1 - t // 2), 1 + lax.rem(t, 2)), [yy(2)], False)
 
+    @pl.when(x == 1)
+    def _():
+        rest(0, 2, three)
+        send_first_row(2)
+
     rest(x, 3, three)
     send_own_row(1)
 
     @pl.when(x == 1)
     def _():
-        rest(0, 2, three)
-        send_first_row(2)
         block([(0, 0), (1, 0)], [yy(2)], False)
 
     @pl.when(x == 0)
@@ -416,13 +418,9 @@
     @pl.when(x == 1)
     def _():
         rest(0, 1, sides)
+        send_first_row(3)
 
     rest(x, 2, sides)
-
-    @pl.when(x == 1)
-    def _():
-        send_first_row(3)
-
     send_own_row(2)
 
     @pl.when(x == 1)
@@ -486,22 +484,27 @@
     def forward(i):
         return move(relay.at[rows[i]], last.at[rows[i]], hs.at[3, 0, i], hs.at[3, 1, i], device(DIRS[i % 2]))
 
-    def product(c):
-        return dot(act[...], wbuf[c], ((1,), (1,))).astype(BF16)
-
-    for c in range(tiles):
-        far[:, c * TILE:(c + 1) * TILE] = product((1 - x_hi) * tiles + c)
+    def product(into, hi, c):
+        at = pl.ds(pl.multiple_of(c * TILE, TILE), TILE)
+        into[:, at] = dot(act[...], wbuf[hi * tiles + c], ((1,), (1,))).astype(BF16)
+
+    for c in range(tiles // 2):
+        product(far, 1 - x_hi, (1 - core) * (tiles // 2) + c)
     for i in range(PIECES):
         swap(i, 0).start()
+    for c in range(tiles // 2):
+        product(far, 1 - x_hi, core * (tiles // 2) + c)
     for i in range(PIECES):
         swap(i, 0).wait_recv()
         mine = far[rows[i], columns(core)].astype(F32)
         stage[rows[i]] = (mine + farb[rows[i]].astype(F32)).astype(BF16)
         hop(i).start()
-    for c in range(tiles):
-        near[:, c * TILE:(c + 1) * TILE] = product(x_hi * tiles + c)
+    for c in range(tiles // 2):
+        product(near, x_hi, (1 - core) * (tiles // 2) + c)
     for i in range(PIECES):
         swap(i, 1).start()
+    for c in range(tiles // 2):
+        product(near, x_hi, core * (tiles // 2) + c)
     for i in range(PIECES):
         hop(i).wait_recv()
         forward(i).start()

time: 77.8 us -> 77.9 us (level)
  no operation moved by 1% of the time
where the time goes in v4:
time: 77.9 us; the launch traced here: 77.8 us
  Pallas kernels  77.1 us (99%)
    pallas_call x1, Pallas kernels, on_device(): pl.pallas_call(fused_kernel, name='attention_backward', out_shape=(jax.Sh...  75.2 us
    pallas_call x1, Pallas kernels, on_device(): pl.pallas_call(hand_over, name='hand_over', out_shape=tuple((jax.ShapeDty...  1.87 us

profile of v4, /device:TPU:1, one launch (start us, length us, event | category | flops | bytes accessed | tf_op | source)
XLA Modules:
  0.0 77.8 jit_solution(15094325017097719350)
XLA Ops:
  0.6 75.2 %attention_backward.1 = (bf16[192,1024]{1,0:T(8,128)(2,1)}, f32[192,128]{1,0:T(8,128)}, f32[192,128]{1,0:T(8,128)}) custom-call(s32[64]{0:T(128)} %count_ref.1, bf16[192,128]{1,0:T(8,128)(2,1)} %k_ref.1, bf16[192,128]{1,0:T(8,128)(2,1)} %v_ref.1, bf16[192,512]{1,0:T(8,128)(2,1)} %q_ref.1, bf16[192,512]{1,0:T(8,128)(2,1)} %g_ref.1, bf16[192,512]{1,0:T(8,128)(2,1)} %o_ref.1, ...), custom_call_target="tpu_custom_call" | custom-call | tf_op jit(solution)/shard_map/attention_backward/pallas_call | solution.py:576
  75.9 1.9 %hand_over.1 = (bf16[192,1024]{1,0:T(8,128)(2,1)}, f32[192,128]{1,0:T(8,128)}, f32[192,128]{1,0:T(8,128)}) custom-call(bf16[192,1024]{1,0:T(8,128)(2,1)} %get-tuple-element.6.refs_0_, f32[192,128]{1,0:T(8,128)} %get-tuple-element.7.refs_1_, f32[192,128]{1,0:T(8,128)} %get-tuple-element.8.refs_2_), custom_call_target="tpu_custom_call" | custom-call | tf_op jit(solution)/shard_map/hand_over/pallas_call | solution.py:609
